TPU v7x, 256 devices: a 2x2x32 block of a 4x8x32 slice. The times are simulated.
256 devices in a mesh: grp: 4 (over y, x), freq: 64 (over z, core).
Axes of the slice: x: 2, y: 2, z: 32, core: 2. Of those that a mesh axis runs over, the one named last changes fastest.
The devices are a block of a 4x8x32 slice.
Arguments:
- kernel: bfloat16 [2, 512, 1024, 1024], P(None, ('grp', 'freq')), parts along dimension 1, may hold values from -0.125 to 0.125
- recorded: float32 [2, 512, 1024, 128], P(None, ('grp', 'freq')), parts along dimension 1, may hold values from -8 to 8
- onset_time: int32 [4096, 128], P(('grp', 'freq')), parts along dimension 0, may hold values from 32 to 256, as said below
Outputs:
- focusing: float32 [256, 4096, 128], P(None, ('grp', 'freq')), parts along dimension 1
There are 4 independent parts, one for each index of `grp`. A program takes and returns all parts, laid end to end along the dimension named above; each array names one. Nothing has to cross between parts.
Inputs may be any that keep to these rules, and one draw needn't show every extreme that they name: `onset_time`: onset sample of the window for each receiver and focal point.
All inputs are finite; a program needn't handle non-finite values.
Results may differ from a plain program's by a relative error of at most 0.012.
Values may be sent and summed in bfloat16 or wider, within the bound.
A program may use at most 64 MiB of HBM per device.

v0:
```python
import functools
import math
import jax
import jax.numpy as jnp
from jax import lax
from jax.sharding import Mesh
from jax.sharding import PartitionSpec as P

NF = 128
ITERS = 2
FREQ = ("freq_0", "freq_1")
GRP_FREQ = ("grp", "freq_0", "freq_1")


def by_axis(shard, axes):
    return functools.reduce(lax.psum, axes, shard)


def dft_tables():
    samples = jnp.arange(2 * NF, dtype=jnp.int32)
    bins = jnp.arange(NF, dtype=jnp.int32)
    phase = (bins[:, None] * samples[None, :] % (2 * NF)).astype(jnp.float32) * (math.pi / NF)
    factor = 1.0 / math.sqrt(NF)
    return (jnp.cos(phase) * factor, jnp.sin(phase) * factor)


def square_sum(values):
    return jnp.sum(values * values)


def joint_total(first, second, third):
    return (by_axis(first, FREQ), by_axis(second, FREQ), by_axis(third, FREQ))


def body(kernel, recorded, onset_time):
    cosine_table, sin_tab = dft_tables()
    rec_local = onset_time.shape[0]
    focal_count = onset_time.shape[1]
    samples = lax.broadcasted_iota(jnp.int32, (2 * NF, rec_local, focal_count), 0)
    keep_mask = (samples < onset_time[None]).astype(jnp.float32)
    kernel_real = kernel[0]
    kernel_imaginary = kernel[1]

    def invert(block_in):
        columns = block_in.shape[3]
        widened = block_in.astype(jnp.float32)
        timed = jnp.dot(cosine_table.T, widened[0].reshape(NF, -1)) - jnp.dot(
            sin_tab.T, widened[1].reshape(NF, -1)
        )
        return timed.reshape(2 * NF, block_in.shape[2], columns)

    def apply_adjoint(resid):
        rounded = resid.astype(jnp.bfloat16)
        update_real = rounded[0]
        update_imaginary = rounded[1]
        z_real = jnp.einsum(
            "hvi,hvg->hig", kernel_real, update_real, preferred_element_type=jnp.float32
        ) + jnp.einsum(
            "hvi,hvg->hig", kernel_imaginary, update_imaginary, preferred_element_type=jnp.float32
        )
        z_imag = jnp.einsum(
            "hvi,hvg->hig", kernel_real, update_imaginary, preferred_element_type=jnp.float32
        ) - jnp.einsum(
            "hvi,hvg->hig", kernel_imaginary, update_real, preferred_element_type=jnp.float32
        )
        image = jnp.stack([z_real, z_imag]).astype(jnp.bfloat16)
        timed = invert(lax.all_to_all(image, FREQ, split_axis=2, concat_axis=1, tiled=True))
        return timed * keep_mask

    model_raw = apply_adjoint(recorded)
    totals = joint_total(square_sum(recorded), square_sum(model_raw), jnp.float32(0.0))
    beta_now = jnp.sqrt(totals[0])
    data_vec = recorded / beta_now
    alpha_now = jnp.sqrt(totals[1]) / beta_now
    model_vec = model_raw / (alpha_now * beta_now)
    search = model_vec
    estimate = jnp.zeros_like(model_vec)
    phibar_now = beta_now
    rhobar_now = alpha_now
    for iteration in range(ITERS):
        flat_part = (model_vec * keep_mask).reshape(2 * NF, -1)
        spec_real = jnp.dot(cosine_table, flat_part)
        spec_imag = -jnp.dot(sin_tab, flat_part)
        spectrum = (
            jnp.stack([spec_real, spec_imag])
            .reshape(2, NF, rec_local, focal_count)
            .astype(jnp.bfloat16)
        )
        multiply_block_in = lax.all_to_all(spectrum, FREQ, split_axis=1, concat_axis=2, tiled=True)
        solution_real = multiply_block_in[0]
        solution_imaginary = multiply_block_in[1]
        y_real = jnp.einsum(
            "ptx,pxi->pti", kernel_real, solution_real, preferred_element_type=jnp.float32
        ) - jnp.einsum(
            "ptx,pxi->pti", kernel_imaginary, solution_imaginary, preferred_element_type=jnp.float32
        )
        y_imag = jnp.einsum(
            "ptx,pxi->pti", kernel_real, solution_imaginary, preferred_element_type=jnp.float32
        ) + jnp.einsum(
            "ptx,pxi->pti", kernel_imaginary, solution_real, preferred_element_type=jnp.float32
        )
        data_raw = jnp.stack([y_real, y_imag]) - alpha_now * data_vec
        image_raw = apply_adjoint(data_raw)
        totals = joint_total(
            square_sum(data_raw), square_sum(image_raw), jnp.sum(image_raw * model_vec)
        )
        beta_now = jnp.sqrt(totals[0])
        data_vec = data_raw / beta_now
        alpha_now = jnp.sqrt(
            totals[1] / (beta_now * beta_now) - 2.0 * totals[2] + beta_now * beta_now
        )
        model_vec = (image_raw / beta_now - beta_now * model_vec) / alpha_now
        rho_now = jnp.sqrt(rhobar_now * rhobar_now + beta_now * beta_now)
        cosine = rhobar_now / rho_now
        sine_part = beta_now / rho_now
        theta_now = sine_part * alpha_now
        rhobar_now = -cosine * alpha_now
        phi_now = cosine * phibar_now
        phibar_now = sine_part * phibar_now
        estimate = estimate + phi_now / rho_now * search
        search = model_vec - theta_now / rho_now * search
    return estimate


def solution(mesh):
    torus = Mesh(mesh.devices.reshape(mesh.shape["grp"], 32, 2), ("grp", "freq_0", "freq_1"))
    placed = (P(None, GRP_FREQ, None, None), P(None, GRP_FREQ, None, None), P(GRP_FREQ, None))
    return jax.shard_map(
        body, mesh=torus, in_specs=placed, out_specs=P(None, GRP_FREQ, None), check_vma=False
    )
```

profile of v0, /device:TPU:37, one launch (start us, length us, event | category | flops | bytes accessed | tf_op | source)
XLA Modules:
  0.0 739.0 jit_solution(18064123041767849132)
XLA Ops:
  0.0 3.5 multiply_reduce_fusion.3
  3.5 4.0 fusion.14
  14.0 141.8 %all_to_all.60 = bf16[2,2,1024,128]{3,1,0,2:T(2,128)(2,1)S(1)} all-to-all(bf16[2,2,1024,128]{3,1,0,2:T(2,128)(2,1)S(1)} %copy.81), channel_id=1, replica_groups=mesh['grp'=4,'freq_0'=32,'freq_1'=2] {'freq_0','freq_1'}, dimensions={2} | all-to-all | bytes 2097152 | tf_op jit(solution)/shard_map/all_to_all | solution.py:67
  158.9 41.1 %all-reduce.1 = (f32[]{:T(128)}, f32[]{:T(128)}) all-reduce(f32[]{:T(128)} %get-tuple-element.29, f32[]{:T(128)} %get-tuple-element.19), channel_id=1, replica_groups=mesh['grp'=4,'freq_0'=32,'freq_1'=2] {'freq_0'}, use_global_device_ids=true, to_apply=%region_1.2 | all-reduce | flops 2 | bytes 16 | tf_op jit(solution)/shard_map/psum | solution.py:16
  200.0 18.1 %all-reduce.3 = (f32[]{:T(128)}, f32[]{:T(128)}) all-reduce(f32[]{:T(128)} %get-tuple-element.10, f32[]{:T(128)} %get-tuple-element.11), channel_id=1, replica_groups=mesh['grp'=4,'freq_0'=32,'freq_1'=2] {'freq_1'}, use_global_device_ids=true, to_apply=%region_2.3 | all-reduce | flops 2 | bytes 16 | tf_op jit(solution)/shard_map/psum | solution.py:16
  223.0 8.3 %all-to-all-start.1 = ((bf16[2,128,16,128]{3,2,0,1:T(8,128)(2,1)}), bf16[2,128,16,128]{3,2,0,1:T(8,128)(2,1)S(1)}, u32[]{:S(2)}, u32[]{:S(2)}) async-start(bf16[2,128,16,128]{3,2,0,1:T(8,128)(2,1)} %pad_maximum_fusion.1), calls=%async_computation.1 | async-start | bytes 2097152 | tf_op jit(solution)/shard_map/all_to_all | solution.py:89
  231.3 2.9 copy.96
  234.2 104.1 %all-to-all-done.1 = bf16[2,128,16,128]{3,2,0,1:T(8,128)(2,1)S(1)} async-done(((bf16[2,128,16,128]{3,2,0,1:T(8,128)(2,1)}), bf16[2,128,16,128]{3,2,0,1:T(8,128)(2,1)S(1)}, u32[]{:S(2)}, u32[]{:S(2)}) %all-to-all-start.1) | async-done | bytes 1048608 | tf_op jit(solution)/shard_map/all_to_all | solution.py:89
  338.7 3.8 fusion.10
  342.6 3.7 fusion.8
  354.3 2.0 copy.101
  356.4 116.7 %all_to_all.61 = bf16[2,2,1024,128]{3,1,0,2:T(2,128)(2,1)S(1)} all-to-all(bf16[2,2,1024,128]{3,1,0,2:T(2,128)(2,1)} %copy.101), channel_id=1, replica_groups=mesh['grp'=4,'freq_0'=32,'freq_1'=2] {'freq_0','freq_1'}, dimensions={2} | all-to-all | bytes 2097152 | tf_op jit(solution)/shard_map/all_to_all | solution.py:67
  474.4 3.3 multiply_reduce_fusion
  477.7 39.7 %all-reduce = (f32[]{:T(128)}, f32[]{:T(128)}, f32[]{:T(128)}) all-reduce(f32[]{:T(128)} %get-tuple-element.17, f32[]{:T(128)} %get-tuple-element.6, f32[]{:T(128)} %get-tuple-element.5), channel_id=1, replica_groups=mesh['grp'=4,'freq_0'=32,'freq_1'=2] {'freq_0'}, use_global_device_ids=true, to_apply=%region_7.8 | all-reduce | flops 3 | bytes 24 | tf_op jit(solution)/shard_map/psum | solution.py:16
  517.4 19.5 %all-reduce.2 = (f32[]{:T(128)}, f32[]{:T(128)}, f32[]{:T(128)}) all-reduce(f32[]{:T(128)} %get-tuple-element.7, f32[]{:T(128)} %get-tuple-element.8, f32[]{:T(128)} %get-tuple-element.9), channel_id=1, replica_groups=mesh['grp'=4,'freq_0'=32,'freq_1'=2] {'freq_1'}, use_global_device_ids=true, to_apply=%region_8.9 | all-reduce | flops 3 | bytes 24 | tf_op jit(solution)/shard_map/psum | solution.py:16
  538.8 2.4 divide_select_fusion
  544.1 7.9 %all-to-all-start.3 = ((bf16[2,128,16,128]{3,2,0,1:T(8,128)(2,1)}), bf16[2,128,16,128]{3,2,0,1:T(8,128)(2,1)S(1)}, u32[]{:S(2)}, u32[]{:S(2)}) async-start(bf16[2,128,16,128]{3,2,0,1:T(8,128)(2,1)} %pad_maximum_fusion.3), calls=%async_computation.3 | async-start | bytes 2097152 | tf_op jit(solution)/shard_map/all_to_all | solution.py:89
  553.9 105.1 %all-to-all-done.3 = bf16[2,128,16,128]{3,2,0,1:T(8,128)(2,1)S(1)} async-done(((bf16[2,128,16,128]{3,2,0,1:T(8,128)(2,1)}), bf16[2,128,16,128]{3,2,0,1:T(8,128)(2,1)S(1)}, u32[]{:S(2)}, u32[]{:S(2)}) %all-to-all-start.3) | async-done | bytes 1048608 | tf_op jit(solution)/shard_map/all_to_all | solution.py:89
  659.4 3.8 fusion.2
  663.3 3.7 fusion
  671.4 41.0 %psum.94 = f32[]{:T(128)} all-reduce(f32[]{:T(128)} %fusion.40), channel_id=1, replica_groups=mesh['grp'=4,'freq_0'=32,'freq_1'=2] {'freq_0'}, use_global_device_ids=true, to_apply=%region_16.17 | all-reduce | flops 1 | bytes 8 | tf_op jit(solution)/shard_map/psum | solution.py:16
  712.5 3.5 copy.149
  716.0 18.1 %psum.95 = f32[]{:T(128)} all-reduce(f32[]{:T(128)} %psum.94), channel_id=1, replica_groups=mesh['grp'=4,'freq_0'=32,'freq_1'=2] {'freq_1'}, use_global_device_ids=true, to_apply=%region_17.18 | all-reduce | flops 1 | bytes 8 | tf_op jit(solution)/shard_map/psum | solution.py:16
  734.9 3.8 multiply_add_fusion
  (70 shorter events, 31.8 us)
Async XLA Ops:
  0.0 7.6 %copy-start = (bf16[2,2,1024,1024]{3,2,1,0:T(8,128)(2,1)S(1)}, bf16[2,2,1024,1024]{3,2,1,0:T(8,128)(2,1)}, u32[]{:S(2)}) copy-start(bf16[2,2,1024,1024]{3,2,1,0:T(8,128)(2,1)} %param.3) | copy-start | bytes 25165828
  156.0 1.1 copy-start.5
  223.0 115.3 %all-to-all-start.1 = ((bf16[2,128,16,128]{3,2,0,1:T(8,128)(2,1)}), bf16[2,128,16,128]{3,2,0,1:T(8,128)(2,1)S(1)}, u32[]{:S(2)}, u32[]{:S(2)}) async-start(bf16[2,128,16,128]{3,2,0,1:T(8,128)(2,1)} %pad_maximum_fusion.1), calls=%async_computation.1 | async-start | bytes 2097152 | tf_op jit(solution)/shard_map/all_to_all | solution.py:89
  338.5 7.8 %slice-start = ((s8[8388608]{0:T(1024)(128)(4,1)}), s8[4194304]{0:T(1024)(128)(4,1)S(1)}, s32[]{:S(2)}) async-start(s8[8388608]{0:T(1024)(128)(4,1)} %bitcast.237), calls=%async_computation.4 | async-start | bytes 8388608
  338.7 7.6 %slice-start.1 = ((s8[8388608]{0:T(1024)(128)(4,1)}), s8[4194304]{0:T(1024)(128)(4,1)S(1)}, s32[]{:S(2)}) async-start(s8[8388608]{0:T(1024)(128)(4,1)} %bitcast.237), calls=%async_computation.5 | async-start | bytes 8388608
  347.9 1.6 copy-start.4
  350.6 1.4 copy-start.1
  544.1 114.9 %all-to-all-start.3 = ((bf16[2,128,16,128]{3,2,0,1:T(8,128)(2,1)}), bf16[2,128,16,128]{3,2,0,1:T(8,128)(2,1)S(1)}, u32[]{:S(2)}, u32[]{:S(2)}) async-start(bf16[2,128,16,128]{3,2,0,1:T(8,128)(2,1)} %pad_maximum_fusion.3), calls=%async_computation.3 | async-start | bytes 2097152 | tf_op jit(solution)/shard_map/all_to_all | solution.py:89
  659.2 7.8 %slice-start.2 = ((s8[8388608]{0:T(1024)(128)(4,1)}), s8[4194304]{0:T(1024)(128)(4,1)S(1)}, s32[]{:S(2)}) async-start(s8[8388608]{0:T(1024)(128)(4,1)} %bitcast.239), calls=%async_computation.6 | async-start | bytes 8388608
  659.4 7.6 %slice-start.3 = ((s8[8388608]{0:T(1024)(128)(4,1)}), s8[4194304]{0:T(1024)(128)(4,1)S(1)}, s32[]{:S(2)}) async-start(s8[8388608]{0:T(1024)(128)(4,1)} %bitcast.239), calls=%async_computation.7 | async-start | bytes 8388608
  668.6 1.6 copy-start.2
  712.5 22.4 %copy-start.3 = (f32[32,8,16,128]{3,2,1,0:T(8,128)S(1)}, f32[32,8,16,128]{3,2,1,0:T(8,128)}, u32[]{:S(2)}) copy-start(f32[32,8,16,128]{3,2,1,0:T(8,128)} %copy.144) | copy-start | bytes 6291460
where the time goes:
time: 747 us; the launch traced here: 739 us
  blocking collectives  436 us (58%)
  waiting for transfers between devices  209 us (28%)
  matrix products  43.9 us (6%)
  starting transfers between devices  16.2 us (2%)
  other arithmetic  14.6 us (2%)
  local copies, waits for them, and re-layouts  13.9 us (2%)
    all_to_all x2, blocking collectives, apply_adjoint(): lax.all_to_all(image, FREQ, split_axis=2, concat_axis=1, tiled=True)  258 us
    all_to_all x2, waiting for transfers between devices, body(): lax.all_to_all(spectrum, FREQ, split_axis=1, concat_axis=2, tiled=True)  209 us
    psum x6, blocking collectives, by_axis(): return functools.reduce(lax.psum, axes, shard)  178 us
    all_to_all x2, starting transfers between devices, body(): lax.all_to_all(spectrum, FREQ, split_axis=1, concat_axis=2, tiled=True)  16.2 us
  transfers between devices with their start and end apart: 2, of which 2 were waited for; matrix products, arithmetic and copies ran while one was open for 1% of the time, Pallas kernels for 0%

commit v1 on v0

--- a/solution.py
+++ b/solution.py
@@ -86,7 +86,10 @@
             .reshape(2, NF, rec_local, focal_count)
             .astype(jnp.bfloat16)
         )
-        multiply_block_in = lax.all_to_all(spectrum, FREQ, split_axis=1, concat_axis=2, tiled=True)
+        multiply_block_in = jnp.concatenate(
+            lax.all_to_all(jnp.stack(jnp.split(spectrum, lax.axis_size(FREQ), axis=1)), FREQ, 0, 0),
+            axis=2,
+        )
         solution_real = multiply_block_in[0]
         solution_imaginary = multiply_block_in[1]
         y_real = jnp.einsum(

time: 747 us -> 822 us (1.10)
  local copies, waits for them, and re-layouts: 13.9 us -> 90.6 us
    unnamed x27 -> x155, local copies, waits for them, and re-layouts: 9.1 us -> 84.7 us
where the time goes in v1:
time: 822 us; the launch traced here: 814 us
  blocking collectives  436 us (53%)
  waiting for transfers between devices  209 us (25%)
  local copies, waits for them, and re-layouts  90.6 us (11%)
  matrix products  44 us (5%)
  starting transfers between devices  16.2 us (2%)
  other arithmetic  12.4 us (2%)
    all_to_all x2, blocking collectives, apply_adjoint(): lax.all_to_all(image, FREQ, split_axis=2, concat_axis=1, tiled=True)  258 us
    all_to_all x2, waiting for transfers between devices, body(): lax.all_to_all(jnp.stack(jnp.split(spectrum, lax.axis_size(FREQ), axis=1)...  209 us
    psum x6, blocking collectives, by_axis(): return functools.reduce(lax.psum, axes, shard)  178 us
    unnamed x155, local copies, waits for them, and re-layouts  84.7 us
  transfers between devices with their start and end apart: 2, of which 2 were waited for; matrix products, arithmetic and copies ran while one was open for 1% of the time, Pallas kernels for 0%

profile of v1, /device:TPU:37, one launch (start us, length us, event | category | flops | bytes accessed | tf_op | source)
XLA Modules:
  0.0 813.6 jit_solution(17452699615599421195)
XLA Ops:
  0.0 3.5 multiply_reduce_fusion.3
  3.5 4.0 fusion.14
  14.0 141.8 %all_to_all.40 = bf16[2,2,1024,128]{3,1,0,2:T(2,128)(2,1)S(1)} all-to-all(bf16[2,2,1024,128]{3,1,0,2:T(2,128)(2,1)S(1)} %copy.178), channel_id=1, replica_groups=mesh['grp'=4,'freq_0'=32,'freq_1'=2] {'freq_0','freq_1'}, dimensions={2} | all-to-all | bytes 2097152 | tf_op jit(solution)/shard_map/all_to_all | solution.py:67
  158.9 41.1 %all-reduce.1 = (f32[]{:T(128)}, f32[]{:T(128)}) all-reduce(f32[]{:T(128)} %get-tuple-element.29, f32[]{:T(128)} %get-tuple-element.19), channel_id=1, replica_groups=mesh['grp'=4,'freq_0'=32,'freq_1'=2] {'freq_0'}, use_global_device_ids=true, to_apply=%region_1.2 | all-reduce | flops 2 | bytes 16 | tf_op jit(solution)/shard_map/psum | solution.py:16
  200.0 18.1 %all-reduce.3 = (f32[]{:T(128)}, f32[]{:T(128)}) all-reduce(f32[]{:T(128)} %get-tuple-element.10, f32[]{:T(128)} %get-tuple-element.11), channel_id=1, replica_groups=mesh['grp'=4,'freq_0'=32,'freq_1'=2] {'freq_1'}, use_global_device_ids=true, to_apply=%region_2.3 | all-reduce | flops 2 | bytes 16 | tf_op jit(solution)/shard_map/psum | solution.py:16
  260.3 8.3 %all-to-all-start.1 = ((bf16[64,2,2,16,128]{4,3,2,1,0:T(8,128)(2,1)}), bf16[64,2,2,16,128]{4,3,2,1,0:T(8,128)(2,1)S(1)}, u32[]{:S(2)}, u32[]{:S(2)}) async-start(bf16[64,2,2,16,128]{4,3,2,1,0:T(8,128)(2,1)} %constant_dynamic-update-slice_fusion), calls=%async_computation.1 | async-start | bytes 2097152 | tf_op jit(solution)/shard_map/all_to_all | solution.py:90
  268.6 2.9 copy.189
  271.4 104.1 %all-to-all-done.1 = bf16[64,2,2,16,128]{4,3,2,1,0:T(8,128)(2,1)S(1)} async-done(((bf16[64,2,2,16,128]{4,3,2,1,0:T(8,128)(2,1)}), bf16[64,2,2,16,128]{4,3,2,1,0:T(8,128)(2,1)S(1)}, u32[]{:S(2)}, u32[]{:S(2)}) %all-to-all-start.1) | async-done | bytes 1048608 | tf_op jit(solution)/shard_map/all_to_all | solution.py:90
  375.9 3.9 fusion.10
  379.8 3.7 fusion.8
  391.6 2.0 copy.194
  393.6 116.7 %all_to_all.41 = bf16[2,2,1024,128]{3,1,0,2:T(2,128)(2,1)S(1)} all-to-all(bf16[2,2,1024,128]{3,1,0,2:T(2,128)(2,1)} %copy.194), channel_id=1, replica_groups=mesh['grp'=4,'freq_0'=32,'freq_1'=2] {'freq_0','freq_1'}, dimensions={2} | all-to-all | bytes 2097152 | tf_op jit(solution)/shard_map/all_to_all | solution.py:67
  511.6 3.3 multiply_reduce_fusion
  514.9 39.7 %all-reduce = (f32[]{:T(128)}, f32[]{:T(128)}, f32[]{:T(128)}) all-reduce(f32[]{:T(128)} %get-tuple-element.17, f32[]{:T(128)} %get-tuple-element.6, f32[]{:T(128)} %get-tuple-element.5), channel_id=1, replica_groups=mesh['grp'=4,'freq_0'=32,'freq_1'=2] {'freq_0'}, use_global_device_ids=true, to_apply=%region_7.8 | all-reduce | flops 3 | bytes 24 | tf_op jit(solution)/shard_map/psum | solution.py:16
  554.6 19.5 %all-reduce.2 = (f32[]{:T(128)}, f32[]{:T(128)}, f32[]{:T(128)}) all-reduce(f32[]{:T(128)} %get-tuple-element.7, f32[]{:T(128)} %get-tuple-element.8, f32[]{:T(128)} %get-tuple-element.9), channel_id=1, replica_groups=mesh['grp'=4,'freq_0'=32,'freq_1'=2] {'freq_1'}, use_global_device_ids=true, to_apply=%region_8.9 | all-reduce | flops 3 | bytes 24 | tf_op jit(solution)/shard_map/psum | solution.py:16
  576.0 2.4 divide_select_fusion
  618.7 7.9 all-to-all-start.3
  628.5 105.1 %all-to-all-done.3 = bf16[64,2,2,16,128]{4,3,2,1,0:T(8,128)(2,1)S(1)} async-done(((bf16[64,2,2,16,128]{4,3,2,1,0:T(8,128)(2,1)}), bf16[64,2,2,16,128]{4,3,2,1,0:T(8,128)(2,1)S(1)}, u32[]{:S(2)}, u32[]{:S(2)}) %all-to-all-start.3) | async-done | bytes 1048608 | tf_op jit(solution)/shard_map/all_to_all | solution.py:90
  734.0 3.9 fusion.2
  737.9 3.7 fusion
  746.0 41.0 %psum.94 = f32[]{:T(128)} all-reduce(f32[]{:T(128)} %fusion.40), channel_id=1, replica_groups=mesh['grp'=4,'freq_0'=32,'freq_1'=2] {'freq_0'}, use_global_device_ids=true, to_apply=%region_16.17 | all-reduce | flops 1 | bytes 8 | tf_op jit(solution)/shard_map/psum | solution.py:16
  787.1 3.5 copy.238
  790.6 18.1 %psum.95 = f32[]{:T(128)} all-reduce(f32[]{:T(128)} %psum.94), channel_id=1, replica_groups=mesh['grp'=4,'freq_0'=32,'freq_1'=2] {'freq_1'}, use_global_device_ids=true, to_apply=%region_17.18 | all-reduce | flops 1 | bytes 8 | tf_op jit(solution)/shard_map/psum | solution.py:16
  809.5 3.8 multiply_add_fusion
  (193 shorter events, 106.4 us)
Async XLA Ops:
  0.0 7.6 copy-start
  156.0 1.1 copy-start.5
  260.3 115.3 %all-to-all-start.1 = ((bf16[64,2,2,16,128]{4,3,2,1,0:T(8,128)(2,1)}), bf16[64,2,2,16,128]{4,3,2,1,0:T(8,128)(2,1)S(1)}, u32[]{:S(2)}, u32[]{:S(2)}) async-start(bf16[64,2,2,16,128]{4,3,2,1,0:T(8,128)(2,1)} %constant_dynamic-update-slice_fusion), calls=%async_computation.1 | async-start | bytes 2097152 | tf_op jit(solution)/shard_map/all_to_all | solution.py:90
  375.6 8.0 slice-start
  375.9 7.6 slice-start.1
  385.1 1.6 copy-start.4
  387.9 1.4 copy-start.1
  618.7 114.9 %all-to-all-start.3 = ((bf16[64,2,2,16,128]{4,3,2,1,0:T(8,128)(2,1)}), bf16[64,2,2,16,128]{4,3,2,1,0:T(8,128)(2,1)S(1)}, u32[]{:S(2)}, u32[]{:S(2)}) async-start(bf16[64,2,2,16,128]{4,3,2,1,0:T(8,128)(2,1)} %constant_dynamic-update-slice_fusion.64), calls=%async_computation.3 | async-start | bytes 2097152 | tf_op jit(solution)/shard_map/all_to_all | solution.py:90
  733.7 8.0 slice-start.2
  734.0 7.6 slice-start.3
  743.2 1.6 copy-start.2
  787.1 22.4 %copy-start.3 = (f32[32,8,16,128]{3,2,1,0:T(8,128)S(1)}, f32[32,8,16,128]{3,2,1,0:T(8,128)}, u32[]{:S(2)}) copy-start(f32[32,8,16,128]{3,2,1,0:T(8,128)} %copy.233) | copy-start | bytes 6291460
